TPU v7x, 1024 devices: a whole 4x8x16 slice. The times are simulated.
1024 devices in a mesh: segment: 16 (over z), tok: 32 (over x, y), mp: 2 (over core).
Axes of the slice: x: 4, y: 8, z: 16, core: 2. Of those that a mesh axis runs over, the one named last changes fastest.
Arguments:
- out_cotangent: bfloat16 [16, 4096, 4096], P('segment', 'tok', 'mp'), may hold values from -6 to 6
- block_output: bfloat16 [16, 4096, 4096], P('segment', 'tok', 'mp'), may hold values from -6 to 6
- router_logits: float32 [16, 4096], P('segment', 'tok'), may hold values from -8 to 8
- keep_flags: int32 [16, 4096], P('segment', 'tok'), may hold values from 0 to 1, as said below
- router_weight: float32 [16, 4096], P('segment', 'mp'), may hold values from -0.09375 to 0.09375
- activated: bfloat16 [16, 512, 14336], P('segment', None, 'tok'), may hold values from -4 to 4
Outputs:
- cotangent_received: bfloat16 [16, 4096, 4096], P('segment', 'tok', 'mp')
- grad_out: bfloat16 [16, 4096, 14336], P('segment', 'mp', 'tok')
Inputs may be any that keep to these rules, and one draw needn't show every extreme that they name: `keep_flags`: in every segment each aligned block of 128 tokens (one device of a group) holds at most 48 active tokens, some block holds exactly 48, and the segment holds exactly 512 active tokens.
All inputs are finite; a program needn't handle non-finite values.
Results may differ from a plain program's by a relative error of at most 0.0049.
Values may be sent and summed in bfloat16 or wider, within the bound.
A program may use at most 32 MiB of HBM per device.

v0:
```python
import jax
import jax.numpy as jnp
from jax import lax
from jax.sharding import Mesh
from jax.sharding import PartitionSpec as P

CAP = 48
TOK = ("tok_0", "tok_1")


def gathered_total(value, axis):
    return lax.all_gather(value, axis).sum(0)


def shifted(value, axis, by):
    devices = lax.axis_size(axis)
    pairs = [(i, i + by) for i in range(devices) if 0 <= i + by < devices]
    return lax.ppermute(value, axis, pairs)


def laid_out(parts, dim):
    dims = list(parts.shape[1:])
    dims[dim] *= parts.shape[0]
    return jnp.moveaxis(parts, 0, dim).reshape(dims)


def copy_for_each(value, axis):
    copies = jnp.broadcast_to(value, (lax.axis_size(axis), *value.shape))
    return lax.all_to_all(copies, axis, split_axis=0, concat_axis=0, tiled=True)


def collect(value, axis, dim):
    return laid_out(copy_for_each(value, axis), dim)


def stacked_from(value, axes, sequence):
    parts = value[None]
    for k in sequence:
        parts = lax.all_gather(parts, axes[k], axis=0, tiled=True)
    current = [lax.axis_size(axes[k]) for k in reversed(sequence)]
    parts = parts.reshape(*current, *value.shape)
    turned = sorted(range(len(sequence)), key=lambda place: sequence[len(sequence) - 1 - place])
    return parts.transpose(*turned, *range(len(sequence), parts.ndim)).reshape(-1, *value.shape)


def gather_axes(value, axes, sequence, dim):
    return laid_out(stacked_from(value, axes, sequence), dim)


def per_device(out_cotangent, block_output, router_logits, keep_flags, router_weight, activated):
    cotangent = out_cotangent[0]
    output = block_output[0]
    logits = router_logits[0]
    keep_row = keep_flags[0]
    router_row = router_weight[0]
    stored = activated[0]
    dy_float = cotangent.astype(jnp.float32)
    gate_value = jax.nn.sigmoid(logits)
    gate_part = jnp.sum(dy_float * output.astype(jnp.float32), axis=1)
    grad_gate = gathered_total(gate_part, "mp")
    grad_score = keep_row.astype(jnp.float32) * grad_gate * gate_value * (1.0 - gate_value)
    dx_tokens = (dy_float + grad_score[:, None] * router_row[None, :]).astype(jnp.bfloat16)
    received = shifted(dx_tokens[None], "segment", -1)
    dz_tokens = (gate_value[:, None] * dy_float).astype(jnp.bfloat16)
    position = jnp.cumsum(keep_row) - 1
    live_count = jnp.sum(keep_row)
    slot_index = jnp.arange(CAP, dtype=jnp.int32)
    chooser = ((position[None, :] == slot_index[:, None]) & (keep_row[None, :] > 0)).astype(
        jnp.bfloat16
    )
    dz_rows = jnp.dot(chooser, dz_tokens, preferred_element_type=jnp.float32).astype(jnp.bfloat16)
    every_count = collect(live_count[None], TOK, 0)
    offsets = jnp.cumsum(every_count) - every_count
    rank_table = offsets[:, None] + slot_index[None, :]
    live_table = (slot_index[None, :] < every_count[:, None]).reshape(-1)
    safe_rank = jnp.where(live_table, rank_table.reshape(-1), 0)
    aligned = jnp.where(live_table[:, None], jnp.take(stored, safe_rank, axis=0), 0)
    all_rows = gather_axes(dz_rows, TOK, (0, 1), 0)
    gradient = lax.dot_general(
        all_rows, aligned, (((0,), (0,)), ((), ())), preferred_element_type=jnp.float32
    )
    return (received, gradient[None].astype(jnp.bfloat16))


def solution(mesh):
    split = Mesh(
        mesh.devices.reshape(mesh.shape["segment"], 4, 8, mesh.shape["mp"]),
        ("segment", "tok_0", "tok_1", "mp"),
    )
    in_specs = (
        P("segment", TOK, "mp"),
        P("segment", TOK, "mp"),
        P("segment", TOK),
        P("segment", TOK),
        P("segment", "mp"),
        P("segment", None, TOK),
    )
    out_specs = (P("segment", TOK, "mp"), P("segment", "mp", TOK))
    return jax.shard_map(
        per_device, mesh=split, in_specs=in_specs, out_specs=out_specs, check_vma=False
    )
```

profile of v0, /device:TPU:1, one launch (start us, length us, event | category | flops | bytes accessed | tf_op | source)
XLA Modules:
  0.0 135.6 jit_solution(2031385048732723613)
XLA Ops:
  7.2 0.0 all-gather.5.cloned.1.call-start
  7.2 1.4 %fusion.7 = f32[128]{0:T(128)S(1)} fusion(bf16[1,128,2048]{2,1,0:T(8,128)(2,1)} %param.6, bf16[1,128,2048]{2,1,0:T(8,128)(2,1)} %param.7), kind=kLoop, calls=%fused_computation.12 | loop fusion | flops 1048448 | bytes 1049088 | tf_op jit(solution)/shard_map/reduce_sum | solution.py:59
  8.6 0.0 copy-start.3
  8.6 0.0 copy-start
  8.6 0.0 copy-start.2
  8.7 15.7 %all-gather.2 = f32[2,1,128]{2,1,0:T(1,128)S(1)} all-gather(f32[1,1,128]{2,1,0:T(1,128)S(1)} %bitcast.45), channel_id=2, replica_groups=mesh['segment'=16,'tok_0'=4,'tok_1'=8,'mp'=2] {'mp'}, dimensions={0}, use_global_device_ids=true | all-gather | bytes 1536 | tf_op jit(solution)/shard_map/all_gather | solution.py:12
  24.4 0.7 compare_bitcast_fusion
  25.0 0.8 copy.22
  25.8 0.2 reduce-window.16
  26.0 0.1 add_reduce_fusion
  26.1 0.7 fusion.20
  26.8 1.4 convolution_convert_fusion.1
  28.1 0.0 copy-start.1
  28.2 11.8 %all-gather.1 = bf16[192,2048]{1,0:T(8,128)(2,1)} all-gather(bf16[48,2048]{1,0:T(8,128)(2,1)S(1)} %convolution_convert_fusion.1), channel_id=3, replica_groups=mesh['segment'=16,'tok_0'=4,'tok_1'=8,'mp'=2] {'tok_0'}, dimensions={0}, use_global_device_ids=true | all-gather | bytes 983040 | tf_op jit(solution)/shard_map/all_gather | solution.py:39
  40.0 0.0 all-gather.5.cloned.1.call-update
  40.0 0.0 copy-done.3
  40.0 0.6 reduce_sum.29
  40.7 1.3 broadcast_in_dim.47
  41.9 3.8 %all-to-all-start = ((s32[32,1,1]{2,1,0:T(1,128)}), s32[32,1,1]{2,1,0:T(1,128)S(1)}, u32[]{:S(2)}, u32[]{:S(2)}) async-start(s32[32,1,1]{2,1,0:T(1,128)} %broadcast_in_dim.47), calls=%async_computation | async-start | bytes 32768 | tf_op jit(solution)/shard_map/all_to_all | solution.py:29
  45.8 0.0 copy-done
  45.8 0.0 copy-done.2
  45.8 0.2 fusion.9
  46.0 1.3 collective-permute-start
  47.3 0.0 copy-done.1
  47.3 0.2 copy.25
  47.5 6.9 %all-to-all-done = s32[32,1,1]{2,1,0:T(1,128)S(1)} async-done(((s32[32,1,1]{2,1,0:T(1,128)}), s32[32,1,1]{2,1,0:T(1,128)S(1)}, u32[]{:S(2)}, u32[]{:S(2)}) %all-to-all-start) | async-done | bytes 160 | tf_op jit(solution)/shard_map/all_to_all | solution.py:29
  54.3 0.1 reduce-window.17
  54.4 0.1 reduce.4
  54.5 0.7 reduce.3
  55.2 0.1 iota_add_fusion
  55.3 0.1 iota_compare_fusion.1
  55.3 0.1 select_n.45
  55.4 0.1 lt.55
  55.5 0.1 add.71
  55.6 4.8 %gather_fusion = bf16[1536,448]{1,0:T(8,128)(2,1)S(1)} fusion(bf16[512,448]{1,0:T(8,128)(2,1)S(1)} %bitcast.38, s32[2048]{0:T(1024)S(1)} %pad_clamp_fusion), kind=kCustom, calls=%fused_computation | custom fusion | bytes 2758656 | tf_op jit(solution)/shard_map/jit(_take)/gather | solution.py:77
  60.5 0.0 collective-permute-done
  60.5 59.5 %all-gather.5.cloned.1.call-done = bf16[32,48,2048]{2,1,0:T(8,128)(2,1)} async-done(((bf16[4,48,2048]{2,1,0:T(8,128)(2,1)}), bf16[32,48,2048]{2,1,0:T(8,128)(2,1)}) %all-gather.5.cloned.1.call-update) | async-done | bytes 6291472 | tf_op jit(solution)/shard_map/all_gather | solution.py:39
  120.0 3.4 %copy.23 = bf16[4,8,48,2048]{3,2,1,0:T(8,128)(2,1)S(1)} copy(bf16[4,8,48,2048]{3,2,0,1:T(8,128)(2,1)} %bitcast.39) | data formatting | bytes 12582912 | tf_op jit(solution)/shard_map/transpose | solution.py:43
  123.3 4.6 %fusion = bf16[1,2048,448]{1,2,0:T(8,128)(2,1)} fusion(bf16[1536,2048]{1,0:T(8,128)(2,1)S(1)} %bitcast.40, bf16[1536,448]{1,0:T(8,128)(2,1)S(1)} %gather_fusion, pred[1536]{0:T(1024)(128)(4,1)S(1)} %compare_and_fusion, pred[1536]{0:T(1024)(128)(4,1)S(1)} %lt.55), kind=kOutput, calls=%fused_computation.2 | convolution fusion | flops 2820866048 | bytes 9505792 | tf_op jit(solution)/shard_map/dot_general | solution.py:79
  128.0 0.8 copy.27
  (5 shorter events, 0.1 us)
Async XLA Ops:
  7.2 112.8 %all-gather.5.cloned.1.call-start = ((), (), s32[]{:S(2)}) async-start(), calls=%async_computation.1 | async-start | bytes 7077888 | tf_op jit(solution)/shard_map/all_gather | solution.py:39
  8.6 31.4 %copy-start.3 = (s32[1,128]{1,0:T(1,128)S(1)}, s32[1,128]{1,0:T(1,128)}, u32[]{:S(2)}) copy-start(s32[1,128]{1,0:T(1,128)} %param.9) | copy-start | bytes 1540
  8.6 37.1 %copy-start = (bf16[1,128,2048]{2,1,0:T(8,128)(2,1)S(1)}, bf16[1,128,2048]{2,1,0:T(8,128)(2,1)}, u32[]{:S(2)}) copy-start(bf16[1,128,2048]{2,1,0:T(8,128)(2,1)} %param.6) | copy-start | bytes 1572868
  8.6 37.1 %copy-start.2 = (f32[1,2048]{1,0:T(1,128)S(1)}, f32[1,2048]{1,0:T(1,128)}, u32[]{:S(2)}) copy-start(f32[1,2048]{1,0:T(1,128)} %param.10) | copy-start | bytes 24580
  28.1 19.1 %copy-start.1 = (bf16[1,512,448]{1,2,0:T(8,128)(2,1)S(1)}, bf16[1,512,448]{1,2,0:T(8,128)(2,1)}, u32[]{:S(2)}) copy-start(bf16[1,512,448]{1,2,0:T(8,128)(2,1)} %param.11) | copy-start | bytes 1376260
  41.9 12.4 %all-to-all-start = ((s32[32,1,1]{2,1,0:T(1,128)}), s32[32,1,1]{2,1,0:T(1,128)S(1)}, u32[]{:S(2)}, u32[]{:S(2)}) async-start(s32[32,1,1]{2,1,0:T(1,128)} %broadcast_in_dim.47), calls=%async_computation | async-start | bytes 32768 | tf_op jit(solution)/shard_map/all_to_all | solution.py:29
  46.0 14.5 %collective-permute-start = (bf16[1,128,2048]{2,1,0:T(8,128)(2,1)S(1)}, bf16[1,128,2048]{2,1,0:T(8,128)(2,1)S(1)}, u32[]{:S(2)}, u32[]{:S(2)}) collective-permute-start(bf16[1,128,2048]{2,1,0:T(8,128)(2,1)S(1)} %fusion.9), channel_id=1, source_target_pairs={{64,0},{128,64},{192,128},{256,192},{320,256},{384,320},{448,384},... | collective-permute-start | bytes 1572872 | tf_op jit(solution)/shard_map/ppermute | solution.py:18
Sparse Core Ops, SparseCore 0:
  40.1 79.7 all-gather.4
where the time goes:
time: 136 us
  waiting for transfers between devices  66.4 us (49%)
  blocking collectives  27.5 us (20%)
  between operations  14.2 us (10%)
  local copies, waits for them, and re-layouts  11.5 us (8%)
  matrix products  5.99 us (4%)
  starting transfers between devices  5.16 us (4%)
  other arithmetic  4.93 us (4%)
    all_gather x1, waiting for transfers between devices, stacked_from(): parts = lax.all_gather(parts, axes[k], axis=0, tiled=True)  59.5 us
    all_gather x1, blocking collectives, gathered_total(): return lax.all_gather(value, axis).sum(0)  15.7 us
    all_gather x1, blocking collectives, stacked_from(): parts = lax.all_gather(parts, axes[k], axis=0, tiled=True)  11.8 us
    all_to_all x1, waiting for transfers between devices, copy_for_each(): return lax.all_to_all(copies, axis, split_axis=0, concat_axis=0, tiled=True)  6.85 us
    gather x1, local copies, waits for them, and re-layouts, per_device(): jnp.take(stored, safe_rank, axis=0)  4.81 us
    dot_general x1, matrix products, per_device(): lax.dot_general(all_rows, aligned, (((0,), (0,)), ((), ())), preferred_el...  4.64 us
    all_to_all x1, starting transfers between devices, copy_for_each(): return lax.all_to_all(copies, axis, split_axis=0, concat_axis=0, tiled=True)  3.83 us
    transpose x1, local copies, waits for them, and re-layouts, stacked_from(): parts.transpose(*turned, *range(len(sequence), parts.ndim))  3.36 us
  transfers between devices with their start and end apart: 3, of which 2 were waited for; matrix products, arithmetic and copies ran while one was open for 6% of the time, Pallas kernels for 0%

commit v1 on v0

v1 whole, which is shorter than its diff:
```python
import functools

import jax
import jax.numpy as jnp
from jax import lax
from jax.experimental import pallas as pl
from jax.experimental.pallas import tpu as pltpu
from jax.sharding import PartitionSpec as P

MESH = pl.DeviceIdType.MESH
NX, NY = 4, 8
GROUP = NX * NY
HALF = 24
DEAD = 64.0
ROWS_A = 16
WIDTH = 64
ACTIVE = 512


def ring_plan():
    size = {"A": ROWS_A * 1024, "B": (WIDTH - ROWS_A) * 1024}
    first = {"A": "x", "B": "y"}
    second = {"A": "y", "B": "x"}
    length = {"x": NX, "y": NY}
    rate, latency = 46.6e3, 2.2

    messages = {}
    for c in "AB":
        n = length[first[c]]
        for s in (1, -1):
            for d in range(1, n // 2 + 1):
                messages[(c, 1, 0, s, d)] = size[c] * (0.5 if d == n // 2 else 1.0)
        m = length[second[c]]
        for e in range(n):
            for s in (1, -1):
                for d in range(1, m // 2 + 1):
                    messages[(c, 2, e, s, d)] = size[c] * (0.5 if d == m // 2 else 1.0)

    def needs(key):
        c, stage, e, s, d = key
        if d > 1:
            return [(c, stage, e, s, d - 1)]
        if stage == 1 or e == 0:
            return []
        n = length[first[c]]
        if e < n // 2:
            return [(c, 1, 0, 1, e)]
        if e > n // 2:
            return [(c, 1, 0, -1, n - e)]
        return [(c, 1, 0, 1, n // 2), (c, 1, 0, -1, n // 2)]

    def axis(key):
        return (first if key[1] == 1 else second)[key[0]]

    def rank(key):
        c, stage, e, s, d = key
        return (stage, 0 if c == "B" else 1, -d)

    free = {(a, s): 0.0 for a in "xy" for s in (1, -1)}
    arrived, waiting = {}, {}
    pending = set(messages)
    order = []
    while pending:
        best = None
        for key in pending:
            if any(k not in arrived for k in needs(key)):
                continue
            ready = max([0.0] + [arrived[k] for k in needs(key)])
            start = max(ready, free[(axis(key), key[3])])
            item = (start, rank(key), key)
            if best is None or item < best:
                best = item
        start, _, key = best
        link = (axis(key), key[3])
        free[link] = start + messages[key] / rate
        arrived[key] = start + messages[key] / rate + latency
        order.append((start, key))
        pending.remove(key)
    steps = []
    done = set()
    for start, key in sorted(order, key=lambda item: item[0]):
        for k in needs(key):
            if k not in done:
                done.add(k)
                steps.append(("wait", k))
        steps.append(("send", key))
    tail = sorted((k for k in messages if k not in done), key=lambda k: arrived[k])
    steps += [("wait", k) for k in tail]
    return steps, {k: i for i, k in enumerate(sorted(messages))}, max(arrived.values())


def wrapped(value, n):
    return lax.rem(value + 2 * n, n)


def kernel(
    cot_hbm, out_hbm, logit_hbm, keep_hbm, router_hbm, act_hbm,
    received_ref, grad_ref,
    cot, other, logit, keep, router, act,
    sent, landed, rows, shifted, part, peer_part, score, next_score, next_router,
    local_sem, all_send, all_recv, ring_send, ring_recv, side_send, side_recv,
):
    segment = lax.axis_index("segment")
    tok = lax.axis_index("tok")
    half = lax.axis_index("mp")
    x, y = tok // NY, lax.rem(tok, NY)
    last = lax.axis_size("segment") - 1

    loads = []
    for i, (src, dst) in enumerate((
        (cot_hbm, cot), (keep_hbm, keep), (logit_hbm, logit),
        (out_hbm, other), (router_hbm, router), (act_hbm, act),
    )):
        copy = pltpu.make_async_copy(src, dst, local_sem.at[i])
        copy.start()
        loads.append(copy)

    barrier = pltpu.get_barrier_semaphore()

    def greet(p, carry):
        to = (segment, lax.rem(tok + p, GROUP), half)
        pl.semaphore_signal(barrier, inc=1, device_id=to, device_id_type=MESH)
        return carry

    lax.fori_loop(1, GROUP, greet, 0)
    pl.semaphore_signal(barrier, inc=1, device_id=(segment, tok, 1 - half), device_id_type=MESH)

    @pl.when(segment > 0)
    def _():
        pl.semaphore_signal(barrier, inc=1, device_id=(segment - 1, tok, half), device_id_type=MESH)

    @pl.when(segment < last)
    def _():
        pl.semaphore_signal(barrier, inc=1, device_id=(segment + 1, tok, half), device_id_type=MESH)

    for copy in loads[:3]:
        copy.wait()
    keep_row = keep[...].astype(jnp.float32)
    gate_row = jax.nn.sigmoid(logit[...])
    upper = (
        lax.broadcasted_iota(jnp.int32, (128, 128), 0) <= lax.broadcasted_iota(jnp.int32, (128, 128), 1)
    ).astype(jnp.bfloat16)
    keep_wide = jnp.broadcast_to(keep_row, (8, 128)).astype(jnp.bfloat16)
    place = jnp.dot(keep_wide, upper, preferred_element_type=jnp.float32)[0:1]
    count = jnp.dot(keep_wide, jnp.ones((128, 128), jnp.bfloat16), preferred_element_type=jnp.float32)[0:1]
    slot = lax.broadcasted_iota(jnp.int32, (2 * HALF, 128), 0).astype(jnp.float32)
    chosen = (jnp.broadcast_to(place, slot.shape) == slot + 1.0) & (jnp.broadcast_to(keep_row, slot.shape) > 0.5)
    chooser = chosen.astype(jnp.float32).astype(jnp.bfloat16)
    gate_slot = jnp.sum(jnp.where(chosen, jnp.broadcast_to(gate_row, slot.shape), 0.0), axis=1, keepdims=True)
    dead = slot >= jnp.broadcast_to(count, slot.shape)
    low = lax.broadcasted_iota(jnp.int32, (HALF, 128), 1) < WIDTH
    for k in range(16):
        picked = jnp.dot(chooser, cot[:, 128 * k : 128 * (k + 1)], preferred_element_type=jnp.float32)
        picked = jnp.where(dead, DEAD, picked * gate_slot)
        top, bottom = picked[:HALF], picked[HALF:]
        sent[2 * k] = jnp.where(low, top, pltpu.roll(bottom, WIDTH, 1)).astype(jnp.bfloat16)
        sent[2 * k + 1] = jnp.where(low, pltpu.roll(top, WIDTH, 1), bottom).astype(jnp.bfloat16)

    ends = (segment > 0).astype(jnp.int32) + (segment < last).astype(jnp.int32)
    pl.semaphore_wait(barrier, GROUP + ends)

    def to_peer(p):
        peer = lax.rem(tok + p, GROUP)
        return pltpu.make_async_remote_copy(
            src_ref=sent.at[peer], dst_ref=landed.at[tok], send_sem=all_send.at[p], recv_sem=all_recv.at[p],
            device_id=(segment, peer, half), device_id_type=MESH,
        )

    def from_peer(p):
        peer = lax.rem(tok + GROUP - p, GROUP)
        return pltpu.make_async_remote_copy(
            src_ref=sent.at[tok], dst_ref=landed.at[peer], send_sem=all_send.at[p], recv_sem=all_recv.at[p],
            device_id=(segment, peer, half), device_id_type=MESH,
        )

    def send_one(p, carry):
        to_peer(p).start()
        return carry

    lax.fori_loop(1, GROUP, send_one, 0)

    def previous(i, src, dst):
        return pltpu.make_async_remote_copy(
            src_ref=src, dst_ref=dst, send_sem=side_send.at[i], recv_sem=side_recv.at[i],
            device_id=(lax.rem(segment + last, last + 1), tok, half), device_id_type=MESH,
        )

    whole = previous(0, cot, shifted)
    loads[4].wait()
    weights = previous(1, router, next_router)

    @pl.when(segment > 0)
    def _():
        whole.start()
        weights.start()

    loads[3].wait()
    total = jnp.zeros((128, 128), jnp.float32)
    for k in range(16):
        cut = slice(128 * k, 128 * (k + 1))
        total += cot[:, cut].astype(jnp.float32) * other[:, cut].astype(jnp.float32)
    part[...] = jnp.broadcast_to(jnp.sum(total.T, axis=0, keepdims=True), (8, 128))
    landed[tok] = sent[tok]
    swap = pltpu.make_async_remote_copy(
        src_ref=part, dst_ref=peer_part, send_sem=side_send.at[3], recv_sem=side_recv.at[3],
        device_id=(segment, tok, 1 - half), device_id_type=MESH,
    )
    swap.start()
    swap.wait()
    grad_gate = part[0:1] + peer_part[0:1]
    score[...] = jnp.broadcast_to(keep_row * grad_gate * gate_row * (1.0 - gate_row), (8, 128))
    scores = previous(2, score, next_score)

    @pl.when(segment > 0)
    def _():
        scores.start()

    def recv_one(p, carry):
        from_peer(p).wait_recv()
        return carry

    lax.fori_loop(1, GROUP, recv_one, 0)

    got = landed[...].astype(jnp.float32)
    k24 = lax.broadcasted_iota(jnp.int32, (GROUP, HALF, 128), 1).astype(jnp.float32)
    live_top = jnp.broadcast_to(got[:, :, 0:1], got.shape) < 0.5 * DEAD
    live_bottom = jnp.broadcast_to(got[:, :, WIDTH : WIDTH + 1], got.shape) < 0.5 * DEAD
    counts = jnp.sum(live_top.astype(jnp.float32) + live_bottom.astype(jnp.float32), axis=1)
    below = (
        lax.broadcasted_iota(jnp.int32, (GROUP, GROUP), 1) < lax.broadcasted_iota(jnp.int32, (GROUP, GROUP), 0)
    ).astype(jnp.bfloat16)
    offset = jnp.dot(below, counts.astype(jnp.bfloat16), preferred_element_type=jnp.float32)
    offset = jnp.broadcast_to(offset.reshape(GROUP, 1, 128), got.shape)
    rank_top = jnp.where(live_top, offset + k24, -1.0).reshape(GROUP * HALF, 128)
    rank_bottom = jnp.where(live_bottom, offset + k24 + HALF, -1.0).reshape(GROUP * HALF, 128)
    lane = lax.broadcasted_iota(jnp.int32, (GROUP * HALF, 128), 1).astype(jnp.float32)
    flipped = got.reshape(GROUP * HALF, 128).T.astype(jnp.bfloat16)
    own = pl.multiple_of(tok * WIDTH, WIDTH)
    for t in range(ACTIVE // 128):
        pick_top = (rank_top == lane + 128.0 * t).astype(jnp.float32).astype(jnp.bfloat16)
        pick_bottom = (rank_bottom == lane + 128.0 * t).astype(jnp.float32).astype(jnp.bfloat16)
        tile = jnp.dot(flipped[:WIDTH], pick_top, preferred_element_type=jnp.float32)
        tile += jnp.dot(flipped[WIDTH:], pick_bottom, preferred_element_type=jnp.float32)
        rows[pl.ds(own, WIDTH), 128 * t : 128 * (t + 1)] = tile.astype(jnp.bfloat16)

    steps, index, _ = ring_plan()

    def block(key, held):
        c, stage, e, s, d = key
        n = {("A", 1): NX, ("A", 2): NY, ("B", 1): NY, ("B", 2): NX}[(c, stage)]
        back = s * (d - 1 + (1 if held else 0))
        along = (x if n == NX else y) - back
        if stage == 1:
            sx, sy = (along, y) if n == NX else (x, along)
        elif c == "A":
            sx, sy = x - e, along
        else:
            sx, sy = along, y - e
        source = wrapped(sx, NX) * NY + wrapped(sy, NY)
        start, size = (0, ROWS_A) if c == "A" else (ROWS_A, WIDTH - ROWS_A)
        at = pl.ds(pl.multiple_of(source * WIDTH + start, 16), size)
        if d < n // 2:
            return rows.at[at]
        return rows.at[at, pl.ds(0 if s == 1 else ACTIVE // 2, ACTIVE // 2)]

    def ring(key, held):
        c, stage, e, s, d = key
        on_x = (c == "A") == (stage == 1)
        if on_x:
            to = wrapped(x + s, NX) * NY + y
        else:
            to = x * NY + wrapped(y + s, NY)
        ref = block(key, held)
        return pltpu.make_async_remote_copy(
            src_ref=ref, dst_ref=ref, send_sem=ring_send.at[index[key]], recv_sem=ring_recv.at[index[key]],
            device_id=(segment, to, half), device_id_type=MESH,
        )

    for what, key in steps:
        if what == "send":
            ring(key, False).start()
        else:
            ring(key, True).wait_recv()

    loads[5].wait()

    def multiply(i, carry):
        at = pl.multiple_of(i * 256, 256)
        product = lax.dot_general(
            act[...], rows[pl.ds(at, 256), :], (((1,), (1,)), ((), ())), preferred_element_type=jnp.float32
        )
        grad_ref[:, pl.ds(at, 256)] = product.astype(jnp.bfloat16)
        return carry

    lax.fori_loop(0, 8, multiply, 0)

    @pl.when(segment < last)
    def _():
        whole.wait_recv()
        weights.wait_recv()
        scores.wait_recv()
        column = jnp.broadcast_to(next_score[0:1], (128, 128)).T
        for k in range(16):
            cut = slice(128 * k, 128 * (k + 1))
            row = jnp.broadcast_to(next_router[:, cut], (128, 128))
            received_ref[:, cut] = (shifted[:, cut].astype(jnp.float32) + column * row).astype(jnp.bfloat16)

    @pl.when(segment == last)
    def _():
        received_ref[...] = jnp.zeros_like(received_ref)

    @pl.when(segment > 0)
    def _():
        whole.wait_send()
        weights.wait_send()
        scores.wait_send()

    def sent_one(p, carry):
        to_peer(p).wait_send()
        return carry

    lax.fori_loop(1, GROUP, sent_one, 0)
    for what, key in steps:
        if what == "send":
            ring(key, False).wait_send()


def per_device(out_cotangent, block_output, router_logits, keep_flags, router_weight, activated):
    anywhere = pl.BlockSpec(memory_space=pltpu.HBM)
    inside = pl.BlockSpec(memory_space=pltpu.VMEM)
    messages = len(ring_plan()[1])
    bf16, f32 = jnp.bfloat16, jnp.float32
    received, gradient = pl.pallas_call(
        kernel,
        out_shape=(jax.ShapeDtypeStruct((128, 2048), bf16), jax.ShapeDtypeStruct((448, 2048), bf16)),
        in_specs=[anywhere] * 6,
        out_specs=(inside, inside),
        scratch_shapes=[
            pltpu.VMEM((128, 2048), bf16),
            pltpu.VMEM((128, 2048), bf16),
            pltpu.VMEM((1, 128), f32),
            pltpu.VMEM((1, 128), jnp.int32),
            pltpu.VMEM((1, 2048), f32),
            pltpu.VMEM((448, 512), bf16),
            pltpu.VMEM((GROUP, HALF, 128), bf16),
            pltpu.VMEM((GROUP, HALF, 128), bf16),
            pltpu.VMEM((GROUP * WIDTH, ACTIVE), bf16),
            pltpu.VMEM((128, 2048), bf16),
            pltpu.VMEM((8, 128), f32),
            pltpu.VMEM((8, 128), f32),
            pltpu.VMEM((8, 128), f32),
            pltpu.VMEM((8, 128), f32),
            pltpu.VMEM((1, 2048), f32),
            pltpu.SemaphoreType.DMA((6,)),
            pltpu.SemaphoreType.DMA((GROUP,)),
            pltpu.SemaphoreType.DMA((GROUP,)),
            pltpu.SemaphoreType.DMA((messages,)),
            pltpu.SemaphoreType.DMA((messages,)),
            pltpu.SemaphoreType.DMA((4,)),
            pltpu.SemaphoreType.DMA((4,)),
        ],
        compiler_params=pltpu.CompilerParams(collective_id=0, has_side_effects=True, vmem_limit_bytes=48 << 20),
    )(
        out_cotangent[0], block_output[0], router_logits, keep_flags, router_weight, activated[0].T,
    )
    return received[None], gradient.T[None]


def solution(mesh):
    in_specs = (
        P("segment", "tok", "mp"),
        P("segment", "tok", "mp"),
        P("segment", "tok"),
        P("segment", "tok"),
        P("segment", "mp"),
        P("segment", None, "tok"),
    )
    out_specs = (P("segment", "tok", "mp"), P("segment", "mp", "tok"))
    return jax.shard_map(per_device, mesh=mesh, in_specs=in_specs, out_specs=out_specs, check_vma=False)
```

time: 136 us -> 59.5 us (0.44)
  the two profiles are of different devices: /device:TPU:1 before, /device:TPU:8 now
where the time goes in v1:
time: 59.5 us; the launch traced here: 59.2 us
  Pallas kernels  51.4 us (86%)
  local copies, waits for them, and re-layouts  7.12 us (12%)
  between operations  0.65 us (1%)
    pallas_call x1, Pallas kernels, per_device(): pl.pallas_call(kernel, out_shape=(jax.ShapeDtypeStruct((128, 2048), bf16)...  51.4 us
    unnamed x14, local copies, waits for them, and re-layouts  7.12 us

profile of v1, /device:TPU:8, one launch (start us, length us, event | category | flops | bytes accessed | tf_op | source)
XLA Modules:
  0.0 59.2 jit_solution(5610640544241569151)
XLA Ops:
  0.6 0.0 copy-start
  0.6 1.0 %copy-done = bf16[1,128,2048]{2,1,0:T(8,128)(2,1)S(1)} copy-done((bf16[1,128,2048]{2,1,0:T(8,128)(2,1)S(1)}, bf16[1,128,2048]{2,1,0:T(8,128)(2,1)}, u32[]{:S(2)}) %copy-start) | copy-done | bytes 524312
  1.7 0.0 copy-start.1
  1.7 1.0 %copy-done.1 = bf16[1,128,2048]{2,1,0:T(8,128)(2,1)S(1)} copy-done((bf16[1,128,2048]{2,1,0:T(8,128)(2,1)S(1)}, bf16[1,128,2048]{2,1,0:T(8,128)(2,1)}, u32[]{:S(2)}) %copy-start.1) | copy-done | bytes 524312
  2.7 0.0 copy-start.2
  2.7 1.0 %copy-done.2 = bf16[1,512,448]{1,2,0:T(8,128)(2,1)S(1)} copy-done((bf16[1,512,448]{1,2,0:T(8,128)(2,1)S(1)}, bf16[1,512,448]{1,2,0:T(8,128)(2,1)}, u32[]{:S(2)}) %copy-start.2) | copy-done | bytes 458776
  3.7 0.0 copy-start.3
  3.7 0.7 %copy-done.3 = f32[1,2048]{1,0:T(1,128)S(1)} copy-done((f32[1,2048]{1,0:T(1,128)S(1)}, f32[1,2048]{1,0:T(1,128)}, u32[]{:S(2)}) %copy-start.3) | copy-done | bytes 8216
  4.4 0.0 copy-start.4
  4.4 0.7 %copy-done.4 = f32[1,128]{1,0:T(1,128)S(1)} copy-done((f32[1,128]{1,0:T(1,128)S(1)}, f32[1,128]{1,0:T(1,128)}, u32[]{:S(2)}) %copy-start.4) | copy-done | bytes 536
  5.1 0.0 copy-start.5
  5.1 0.7 %copy-done.5 = s32[1,128]{1,0:T(1,128)S(1)} copy-done((s32[1,128]{1,0:T(1,128)S(1)}, s32[1,128]{1,0:T(1,128)}, u32[]{:S(2)}) %copy-start.5) | copy-done | bytes 536
  5.7 51.4 %shard_map.77 = (bf16[128,2048]{1,0:T(8,128)(2,1)S(1)}, bf16[448,2048]{1,0:T(8,128)(2,1)S(1)}) custom-call(bf16[128,2048]{1,0:T(8,128)(2,1)S(1)} %bitcast.11, bf16[128,2048]{1,0:T(8,128)(2,1)S(1)} %bitcast.12, f32[1,128]{1,0:T(1,128)S(1)} %copy-done.4, s32[1,128]{1,0:T(1,128)S(1)} %copy-done.5, f32[1,2048]{1,0:T(1,128)S(1)} %copy-done.3, ...), custom_call_target="tpu_custom_call" | custom-call | tf_op jit(solution)/shard_map/pallas_call | solution.py:333
  57.2 0.8 %copy.10 = bf16[1,128,2048]{2,1,0:T(8,128)(2,1)} copy(bf16[1,128,2048]{2,1,0:T(8,128)(2,1)S(1)} %bitcast.10) | data formatting | bytes 1048576
  58.0 1.2 %copy.11 = bf16[1,2048,448]{1,2,0:T(8,128)(2,1)} copy(bf16[1,2048,448]{1,2,0:T(8,128)(2,1)S(1)} %bitcast.9) | data formatting | bytes 3670016
Async XLA Ops:
  0.6 1.0 %copy-start = (bf16[1,128,2048]{2,1,0:T(8,128)(2,1)S(1)}, bf16[1,128,2048]{2,1,0:T(8,128)(2,1)}, u32[]{:S(2)}) copy-start(bf16[1,128,2048]{2,1,0:T(8,128)(2,1)} %param.6) | copy-start | bytes 1572868
  1.7 1.0 %copy-start.1 = (bf16[1,128,2048]{2,1,0:T(8,128)(2,1)S(1)}, bf16[1,128,2048]{2,1,0:T(8,128)(2,1)}, u32[]{:S(2)}) copy-start(bf16[1,128,2048]{2,1,0:T(8,128)(2,1)} %param.7) | copy-start | bytes 1572868
  2.7 1.0 %copy-start.2 = (bf16[1,512,448]{1,2,0:T(8,128)(2,1)S(1)}, bf16[1,512,448]{1,2,0:T(8,128)(2,1)}, u32[]{:S(2)}) copy-start(bf16[1,512,448]{1,2,0:T(8,128)(2,1)} %param.11) | copy-start | bytes 1376260
  3.7 0.7 %copy-start.3 = (f32[1,2048]{1,0:T(1,128)S(1)}, f32[1,2048]{1,0:T(1,128)}, u32[]{:S(2)}) copy-start(f32[1,2048]{1,0:T(1,128)} %router_hbm.1) | copy-start | bytes 24580
  4.4 0.7 %copy-start.4 = (f32[1,128]{1,0:T(1,128)S(1)}, f32[1,128]{1,0:T(1,128)}, u32[]{:S(2)}) copy-start(f32[1,128]{1,0:T(1,128)} %logit_hbm.1) | copy-start | bytes 1540
  5.1 0.7 %copy-start.5 = (s32[1,128]{1,0:T(1,128)S(1)}, s32[1,128]{1,0:T(1,128)}, u32[]{:S(2)}) copy-start(s32[1,128]{1,0:T(1,128)} %keep_hbm.1) | copy-start | bytes 1540

commit v2 on v1

--- a/solution.py
+++ b/solution.py
@@ -12,7 +12,7 @@
 GROUP = NX * NY
 HALF = 24
 DEAD = 64.0
-ROWS_A = 16
+ROWS_A = 24
 WIDTH = 64
 ACTIVE = 512
 
@@ -22,7 +22,7 @@
     first = {"A": "x", "B": "y"}
     second = {"A": "y", "B": "x"}
     length = {"x": NX, "y": NY}
-    rate, latency = 46.6e3, 2.2
+    rate, latency = 46.6e3, 1.9
 
     messages = {}
     for c in "AB":
@@ -52,9 +52,17 @@
     def axis(key):
         return (first if key[1] == 1 else second)[key[0]]
 
+    after = {key: [] for key in messages}
+    for key in messages:
+        for k in needs(key):
+            after[k].append(key)
+
+    @functools.cache
+    def depth(key):
+        return messages[key] / rate + latency + max([depth(k) for k in after[key]], default=0.0)
+
     def rank(key):
-        c, stage, e, s, d = key
-        return (stage, 0 if c == "B" else 1, -d)
+        return -depth(key)
 
     free = {(a, s): 0.0 for a in "xy" for s in (1, -1)}
     arrived, waiting = {}, {}
@@ -85,8 +93,9 @@
                 steps.append(("wait", k))
         steps.append(("send", key))
     tail = sorted((k for k in messages if k not in done), key=lambda k: arrived[k])
+    head = len(steps)
     steps += [("wait", k) for k in tail]
-    return steps, {k: i for i, k in enumerate(sorted(messages))}, max(arrived.values())
+    return steps, head, {k: i for i, k in enumerate(sorted(messages))}, max(arrived.values())
 
 
 def wrapped(value, n):
@@ -94,10 +103,10 @@
 
 
 def kernel(
-    cot_hbm, out_hbm, logit_hbm, keep_hbm, router_hbm, act_hbm,
-    received_ref, grad_ref,
-    cot, other, logit, keep, router, act,
-    sent, landed, rows, shifted, part, peer_part, score, next_score, next_router,
+    cot_hbm, out_hbm, logit_hbm, keep_hbm, router_hbm,
+    received_ref, rows,
+    cot, other, logit, keep, router,
+    sent, landed, shifted, part, peer_part, score, next_score, next_router,
     local_sem, all_send, all_recv, ring_send, ring_recv, side_send, side_recv,
 ):
     segment = lax.axis_index("segment")
@@ -109,7 +118,7 @@
     loads = []
     for i, (src, dst) in enumerate((
         (cot_hbm, cot), (keep_hbm, keep), (logit_hbm, logit),
-        (out_hbm, other), (router_hbm, router), (act_hbm, act),
+        (out_hbm, other), (router_hbm, router),
     )):
         copy = pltpu.make_async_copy(src, dst, local_sem.at[i])
         copy.start()
@@ -117,21 +126,24 @@
 
     barrier = pltpu.get_barrier_semaphore()
 
-    def greet(p, carry):
-        to = (segment, lax.rem(tok + p, GROUP), half)
-        pl.semaphore_signal(barrier, inc=1, device_id=to, device_id_type=MESH)
-        return carry
-
-    lax.fori_loop(1, GROUP, greet, 0)
-    pl.semaphore_signal(barrier, inc=1, device_id=(segment, tok, 1 - half), device_id_type=MESH)
-
-    @pl.when(segment > 0)
-    def _():
-        pl.semaphore_signal(barrier, inc=1, device_id=(segment - 1, tok, half), device_id_type=MESH)
+    peers = sorted(
+        ((dx, dy) for dx in range(NX) for dy in range(NY) if dx or dy),
+        key=lambda at: -(min(at[0], NX - at[0]) + min(at[1], NY - at[1])),
+    )
+
+    def away(at, sign):
+        return wrapped(x + sign * at[0], NX) * NY + wrapped(y + sign * at[1], NY)
+
+    for at in peers:
+        pl.semaphore_signal(barrier, inc=1, device_id=(segment, away(at, 1), half), device_id_type=MESH)
 
     @pl.when(segment < last)
     def _():
         pl.semaphore_signal(barrier, inc=1, device_id=(segment + 1, tok, half), device_id_type=MESH)
+
+    @pl.when(half == 0)
+    def _():
+        pl.semaphore_signal(barrier, inc=1, device_id=(segment, tok, 1), device_id_type=MESH)
 
     for copy in loads[:3]:
         copy.wait()
@@ -156,28 +168,18 @@
         sent[2 * k] = jnp.where(low, top, pltpu.roll(bottom, WIDTH, 1)).astype(jnp.bfloat16)
         sent[2 * k + 1] = jnp.where(low, pltpu.roll(top, WIDTH, 1), bottom).astype(jnp.bfloat16)
 
-    ends = (segment > 0).astype(jnp.int32) + (segment < last).astype(jnp.int32)
-    pl.semaphore_wait(barrier, GROUP + ends)
-
-    def to_peer(p):
-        peer = lax.rem(tok + p, GROUP)
+    pl.semaphore_wait(barrier, GROUP - 1 + (segment > 0).astype(jnp.int32) + half)
+
+    def exchange(at, sign):
+        peer, i = away(at, sign), at[0] * NY + at[1]
         return pltpu.make_async_remote_copy(
-            src_ref=sent.at[peer], dst_ref=landed.at[tok], send_sem=all_send.at[p], recv_sem=all_recv.at[p],
+            src_ref=sent.at[peer if sign > 0 else tok], dst_ref=landed.at[tok if sign > 0 else peer],
+            send_sem=all_send.at[i], recv_sem=all_recv.at[i],
             device_id=(segment, peer, half), device_id_type=MESH,
         )
 
-    def from_peer(p):
-        peer = lax.rem(tok + GROUP - p, GROUP)
-        return pltpu.make_async_remote_copy(
-            src_ref=sent.at[tok], dst_ref=landed.at[peer], send_sem=all_send.at[p], recv_sem=all_recv.at[p],
-            device_id=(segment, peer, half), device_id_type=MESH,
-        )
-
-    def send_one(p, carry):
-        to_peer(p).start()
-        return carry
-
-    lax.fori_loop(1, GROUP, send_one, 0)
+    for at in peers:
+        exchange(at, 1).start()
 
     def previous(i, src, dst):
         return pltpu.make_async_remote_copy(
@@ -205,21 +207,33 @@
         src_ref=part, dst_ref=peer_part, send_sem=side_send.at[3], recv_sem=side_recv.at[3],
         device_id=(segment, tok, 1 - half), device_id_type=MESH,
     )
-    swap.start()
-    swap.wait()
-    grad_gate = part[0:1] + peer_part[0:1]
-    score[...] = jnp.broadcast_to(keep_row * grad_gate * gate_row * (1.0 - gate_row), (8, 128))
+
+    @pl.when(half == 1)
+    def _():
+        swap.start()
+
     scores = previous(2, score, next_score)
 
-    @pl.when(segment > 0)
-    def _():
-        scores.start()
-
-    def recv_one(p, carry):
-        from_peer(p).wait_recv()
-        return carry
-
-    lax.fori_loop(1, GROUP, recv_one, 0)
+    def answer():
+        @pl.when(half == 0)
+        def _():
+            swap.wait_recv()
+            swap.start()
+
+    def tell():
+        @pl.when(half == 1)
+        def _():
+            swap.wait_recv()
+
+        grad_gate = part[0:1] + peer_part[0:1]
+        score[...] = jnp.broadcast_to(keep_row * grad_gate * gate_row * (1.0 - gate_row), (8, 128))
+
+        @pl.when(segment > 0)
+        def _():
+            scores.start()
+
+    for at in peers:
+        exchange(at, -1).wait_recv()
 
     got = landed[...].astype(jnp.float32)
     k24 = lax.broadcasted_iota(jnp.int32, (GROUP, HALF, 128), 1).astype(jnp.float32)
@@ -243,7 +257,7 @@
         tile += jnp.dot(flipped[WIDTH:], pick_bottom, preferred_element_type=jnp.float32)
         rows[pl.ds(own, WIDTH), 128 * t : 128 * (t + 1)] = tile.astype(jnp.bfloat16)
 
-    steps, index, _ = ring_plan()
+    steps, head, index, _ = ring_plan()
 
     def block(key, held):
         c, stage, e, s, d = key
@@ -258,7 +272,7 @@
             sx, sy = along, y - e
         source = wrapped(sx, NX) * NY + wrapped(sy, NY)
         start, size = (0, ROWS_A) if c == "A" else (ROWS_A, WIDTH - ROWS_A)
-        at = pl.ds(pl.multiple_of(source * WIDTH + start, 16), size)
+        at = pl.ds(pl.multiple_of(source * WIDTH + start, 8), size)
         if d < n // 2:
             return rows.at[at]
         return rows.at[at, pl.ds(0 if s == 1 else ACTIVE // 2, ACTIVE // 2)]
@@ -276,38 +290,33 @@
             device_id=(segment, to, half), device_id_type=MESH,
         )
 
-    for what, key in steps:
+    def receive():
+        @pl.when(segment < last)
+        def _():
+            whole.wait_recv()
+            weights.wait_recv()
+            scores.wait_recv()
+            column = jnp.broadcast_to(next_score[0:1], (128, 128)).T
+            for k in range(16):
+                cut = slice(128 * k, 128 * (k + 1))
+                row = jnp.broadcast_to(next_router[:, cut], (128, 128))
+                received_ref[:, cut] = (shifted[:, cut].astype(jnp.float32) + column * row).astype(jnp.bfloat16)
+
+        @pl.when(segment == last)
+        def _():
+            received_ref[...] = jnp.zeros_like(received_ref)
+
+    for i, (what, key) in enumerate(steps):
+        if i == head // 4:
+            answer()
+        if i == head // 2:
+            tell()
+        if i == head:
+            receive()
         if what == "send":
             ring(key, False).start()
         else:
             ring(key, True).wait_recv()
-
-    loads[5].wait()
-
-    def multiply(i, carry):
-        at = pl.multiple_of(i * 256, 256)
-        product = lax.dot_general(
-            act[...], rows[pl.ds(at, 256), :], (((1,), (1,)), ((), ())), preferred_element_type=jnp.float32
-        )
-        grad_ref[:, pl.ds(at, 256)] = product.astype(jnp.bfloat16)
-        return carry
-
-    lax.fori_loop(0, 8, multiply, 0)
-
-    @pl.when(segment < last)
-    def _():
-        whole.wait_recv()
-        weights.wait_recv()
-        scores.wait_recv()
-        column = jnp.broadcast_to(next_score[0:1], (128, 128)).T
-        for k in range(16):
-            cut = slice(128 * k, 128 * (k + 1))
-            row = jnp.broadcast_to(next_router[:, cut], (128, 128))
-            received_ref[:, cut] = (shifted[:, cut].astype(jnp.float32) + column * row).astype(jnp.bfloat16)
-
-    @pl.when(segment == last)
-    def _():
-        received_ref[...] = jnp.zeros_like(received_ref)
 
     @pl.when(segment > 0)
     def _():
@@ -315,25 +324,44 @@
         weights.wait_send()
         scores.wait_send()
 
-    def sent_one(p, carry):
-        to_peer(p).wait_send()
-        return carry
-
-    lax.fori_loop(1, GROUP, sent_one, 0)
+    swap.wait_send()
+    for at in peers:
+        exchange(at, 1).wait_send()
     for what, key in steps:
         if what == "send":
             ring(key, False).wait_send()
 
 
+def finish(received_ref, rows, act, received_hbm, grad_hbm, grad, sems):
+    first = pltpu.make_async_copy(received_ref, received_hbm, sems.at[8])
+    first.start()
+    copies = [first]
+    for i in range(8):
+        cut = slice(256 * i, 256 * (i + 1))
+        product = lax.dot_general(
+            act[...], rows[cut, :], (((1,), (1,)), ((), ())), preferred_element_type=jnp.float32
+        )
+        grad[i] = product.astype(jnp.bfloat16)
+        copy = pltpu.make_async_copy(grad.at[i], grad_hbm.at[:, cut], sems.at[i])
+        copy.start()
+        copies.append(copy)
+    for copy in copies:
+        copy.wait()
+
+
 def per_device(out_cotangent, block_output, router_logits, keep_flags, router_weight, activated):
     anywhere = pl.BlockSpec(memory_space=pltpu.HBM)
     inside = pl.BlockSpec(memory_space=pltpu.VMEM)
-    messages = len(ring_plan()[1])
+    messages = len(ring_plan()[2])
     bf16, f32 = jnp.bfloat16, jnp.float32
-    received, gradient = pl.pallas_call(
+    far = [
+        pltpu.with_memory_space_constraint(a, pltpu.HBM)
+        for a in (out_cotangent[0], block_output[0], router_logits, keep_flags, router_weight)
+    ]
+    received, rows = pl.pallas_call(
         kernel,
-        out_shape=(jax.ShapeDtypeStruct((128, 2048), bf16), jax.ShapeDtypeStruct((448, 2048), bf16)),
-        in_specs=[anywhere] * 6,
+        out_shape=(jax.ShapeDtypeStruct((128, 2048), bf16), jax.ShapeDtypeStruct((GROUP * WIDTH, ACTIVE), bf16)),
+        in_specs=[anywhere] * 5,
         out_specs=(inside, inside),
         scratch_shapes=[
             pltpu.VMEM((128, 2048), bf16),
@@ -341,17 +369,15 @@
             pltpu.VMEM((1, 128), f32),
             pltpu.VMEM((1, 128), jnp.int32),
             pltpu.VMEM((1, 2048), f32),
-            pltpu.VMEM((448, 512), bf16),
             pltpu.VMEM((GROUP, HALF, 128), bf16),
             pltpu.VMEM((GROUP, HALF, 128), bf16),
-            pltpu.VMEM((GROUP * WIDTH, ACTIVE), bf16),
             pltpu.VMEM((128, 2048), bf16),
             pltpu.VMEM((8, 128), f32),
             pltpu.VMEM((8, 128), f32),
             pltpu.VMEM((8, 128), f32),
             pltpu.VMEM((8, 128), f32),
             pltpu.VMEM((1, 2048), f32),
-            pltpu.SemaphoreType.DMA((6,)),
+            pltpu.SemaphoreType.DMA((5,)),
             pltpu.SemaphoreType.DMA((GROUP,)),
             pltpu.SemaphoreType.DMA((GROUP,)),
             pltpu.SemaphoreType.DMA((messages,)),
@@ -360,9 +386,17 @@
             pltpu.SemaphoreType.DMA((4,)),
         ],
         compiler_params=pltpu.CompilerParams(collective_id=0, has_side_effects=True, vmem_limit_bytes=48 << 20),
-    )(
-        out_cotangent[0], block_output[0], router_logits, keep_flags, router_weight, activated[0].T,
-    )
+        cost_estimate=pl.CostEstimate(flops=20_000_000_000, bytes_accessed=2 << 20, transcendentals=0),
+    )(*far)
+    received, gradient = pl.pallas_call(
+        finish,
+        out_shape=(jax.ShapeDtypeStruct((128, 2048), bf16), jax.ShapeDtypeStruct((448, 2048), bf16)),
+        in_specs=[inside] * 3,
+        out_specs=(anywhere, anywhere),
+        scratch_shapes=[pltpu.VMEM((8, 448, 256), bf16), pltpu.SemaphoreType.DMA((9,))],
+        compiler_params=pltpu.CompilerParams(vmem_limit_bytes=48 << 20),
+        cost_estimate=pl.CostEstimate(flops=1_000_000_000, bytes_accessed=5 << 20, transcendentals=0),
+    )(received, rows, activated[0].T)
     return received[None], gradient.T[None]
 
 

time: 59.5 us -> 49.5 us (0.83)
  local copies, waits for them, and re-layouts: 7.12 us -> 0.01 us
  Pallas kernels: 51.4 us -> 48.7 us
    unnamed x14 -> x2, local copies, waits for them, and re-layouts: 7.12 us -> 0.01 us
    pallas_call x1, Pallas kernels: 51.4 us -> 46.6 us  [per_device(): pl.pallas_call(kernel, out_shape=(jax.ShapeDtypeStruct((128, 2048), bf16)...]
    pallas_call x0 -> x1, Pallas kernels: none -> 2.04 us  [per_device(): pl.pallas_call(finish, out_shape=(jax.ShapeDtypeStruct((128, 2048), bf16)...]
where the time goes in v2:
time: 49.5 us; the launch traced here: 49.3 us
  Pallas kernels  48.7 us (98%)
  between operations  0.66 us (1%)
    pallas_call x1, Pallas kernels, per_device(): pl.pallas_call(kernel, out_shape=(jax.ShapeDtypeStruct((128, 2048), bf16)...  46.6 us
    pallas_call x1, Pallas kernels, per_device(): pl.pallas_call(finish, out_shape=(jax.ShapeDtypeStruct((128, 2048), bf16)...  2.04 us

profile of v2, /device:TPU:8, one launch (start us, length us, event | category | flops | bytes accessed | tf_op | source)
XLA Modules:
  0.0 49.3 jit_solution(3419047432091958955)
XLA Ops:
  0.6 0.0 copy-start
  0.6 46.6 %shard_map.77 = (bf16[128,2048]{1,0:T(8,128)(2,1)S(1)}, bf16[2048,512]{1,0:T(8,128)(2,1)S(1)}) custom-call(bf16[128,2048]{1,0:T(8,128)(2,1)} %bitcast.10, bf16[128,2048]{1,0:T(8,128)(2,1)} %bitcast.11, f32[1,128]{1,0:T(1,128)} %logit_hbm.1, s32[1,128]{1,0:T(1,128)} %keep_hbm.1, f32[1,2048]{1,0:T(1,128)} %router_hbm.1), custom_call_target="tpu_custom_call" | custom-call | flops 20000000000 | bytes 2097152 | tf_op jit(solution)/shard_map/pallas_call | solution.py:361
  47.3 0.0 copy-done
  47.3 2.0 %shard_map.78 = (bf16[128,2048]{1,0:T(8,128)(2,1)}, bf16[448,2048]{1,0:T(8,128)(2,1)}) custom-call(bf16[128,2048]{1,0:T(8,128)(2,1)S(1)} %get-tuple-element.6.received_ref, bf16[2048,512]{1,0:T(8,128)(2,1)S(1)} %get-tuple-element.7.rows, bf16[448,512]{1,0:T(8,128)(2,1)S(1)} %bitcast.9), custom_call_target="tpu_custom_call" | custom-call | flops 1000000000 | bytes 5242880 | tf_op jit(solution)/shard_map/pallas_call | solution.py:391
Async XLA Ops:
  0.6 46.6 %copy-start = (bf16[1,512,448]{1,2,0:T(8,128)(2,1)S(1)}, bf16[1,512,448]{1,2,0:T(8,128)(2,1)}, u32[]{:S(2)}) copy-start(bf16[1,512,448]{1,2,0:T(8,128)(2,1)} %param.11) | copy-start | bytes 1376260

commit v3 on v2

--- a/solution.py
+++ b/solution.py
@@ -17,84 +17,76 @@
 ACTIVE = 512
 
 
+SPLIT = {"A": 2, "B": 2}
+PARENT = {
+    ("A", 1): {1: 0, 2: 1},
+    ("A", 2): {1: 0, 2: 1, 3: 2, 4: 2},
+    ("B", 1): {1: 0, 2: 0, 3: 2, 4: 2},
+    ("B", 2): {1: 0, 2: 1},
+}
+
+
+@functools.cache
 def ring_plan():
-    size = {"A": ROWS_A * 1024, "B": (WIDTH - ROWS_A) * 1024}
-    first = {"A": "x", "B": "y"}
-    second = {"A": "y", "B": "x"}
-    length = {"x": NX, "y": NY}
-    rate, latency = 46.6e3, 1.9
-
-    messages = {}
+    rate, latency, hop = 46.6e3, 2.6, 0.75
+    size = {"A": ROWS_A * 1024 / SPLIT["A"], "B": (WIDTH - ROWS_A) * 1024 / SPLIT["B"]}
+    messages, needs = {}, {}
     for c in "AB":
-        n = length[first[c]]
-        for s in (1, -1):
-            for d in range(1, n // 2 + 1):
-                messages[(c, 1, 0, s, d)] = size[c] * (0.5 if d == n // 2 else 1.0)
-        m = length[second[c]]
-        for e in range(n):
-            for s in (1, -1):
-                for d in range(1, m // 2 + 1):
-                    messages[(c, 2, e, s, d)] = size[c] * (0.5 if d == m // 2 else 1.0)
-
-    def needs(key):
-        c, stage, e, s, d = key
-        if d > 1:
-            return [(c, stage, e, s, d - 1)]
-        if stage == 1 or e == 0:
-            return []
-        n = length[first[c]]
-        if e < n // 2:
-            return [(c, 1, 0, 1, e)]
-        if e > n // 2:
-            return [(c, 1, 0, -1, n - e)]
-        return [(c, 1, 0, 1, n // 2), (c, 1, 0, -1, n // 2)]
-
-    def axis(key):
-        return (first if key[1] == 1 else second)[key[0]]
-
+        n, m = (NX, NY) if c == "A" else (NY, NX)
+        for u in range(SPLIT[c]):
+            for stage, ring, offsets in ((1, n, (0,)), (2, m, range(n))):
+                for e in offsets:
+                    if stage == 1 or e == 0:
+                        base = []
+                    elif e < n // 2:
+                        base = [(c, u, 1, 0, 1, e)]
+                    elif e > n // 2:
+                        base = [(c, u, 1, 0, -1, n - e)]
+                    else:
+                        base = [(c, u, 1, 0, 1, e), (c, u, 1, 0, -1, e)]
+                    for s in (1, -1):
+                        for d in range(1, ring // 2 + 1):
+                            key, parent = (c, u, stage, e, s, d), PARENT[c, stage][d]
+                            messages[key] = (size[c] * (0.5 if d == ring // 2 else 1.0), d - parent)
+                            needs[key] = [(c, u, stage, e, s, parent)] if parent else base
     after = {key: [] for key in messages}
     for key in messages:
-        for k in needs(key):
+        for k in needs[key]:
             after[k].append(key)
 
     @functools.cache
     def depth(key):
-        return messages[key] / rate + latency + max([depth(k) for k in after[key]], default=0.0)
-
-    def rank(key):
-        return -depth(key)
-
-    free = {(a, s): 0.0 for a in "xy" for s in (1, -1)}
-    arrived, waiting = {}, {}
+        nbytes, hops = messages[key]
+        own = nbytes * hops / rate + latency + hop * (hops - 1)
+        return own + max([depth(k) for k in after[key]], default=0.0)
+
+    def link(key):
+        return ((key[0] == "A") == (key[2] == 1), key[4])
+
+    free, arrived, order = {}, {}, []
     pending = set(messages)
-    order = []
     while pending:
         best = None
         for key in pending:
-            if any(k not in arrived for k in needs(key)):
-                continue
-            ready = max([0.0] + [arrived[k] for k in needs(key)])
-            start = max(ready, free[(axis(key), key[3])])
-            item = (start, rank(key), key)
-            if best is None or item < best:
-                best = item
+            if all(k in arrived for k in needs[key]):
+                ready = max([0.0] + [arrived[k] for k in needs[key]])
+                item = (max(ready, free.get(link(key), 0.0)), -depth(key), key)
+                best = item if best is None else min(best, item)
         start, _, key = best
-        link = (axis(key), key[3])
-        free[link] = start + messages[key] / rate
-        arrived[key] = start + messages[key] / rate + latency
+        nbytes, hops = messages[key]
+        free[link(key)] = start + nbytes * hops / rate
+        arrived[key] = free[link(key)] + latency + hop * (hops - 1)
         order.append((start, key))
         pending.remove(key)
-    steps = []
-    done = set()
+    steps, done = [], set()
     for start, key in sorted(order, key=lambda item: item[0]):
-        for k in needs(key):
+        for k in needs[key]:
             if k not in done:
                 done.add(k)
                 steps.append(("wait", k))
         steps.append(("send", key))
-    tail = sorted((k for k in messages if k not in done), key=lambda k: arrived[k])
     head = len(steps)
-    steps += [("wait", k) for k in tail]
+    steps += [("wait", k) for k in sorted((k for k in messages if k not in done), key=lambda k: arrived[k])]
     return steps, head, {k: i for i, k in enumerate(sorted(messages))}, max(arrived.values())
 
 
@@ -107,7 +99,7 @@
     received_ref, rows,
     cot, other, logit, keep, router,
     sent, landed, shifted, part, peer_part, score, next_score, next_router,
-    local_sem, all_send, all_recv, ring_send, ring_recv, side_send, side_recv,
+    local_sem, all_send, all_recv, ring_send, ring_recv, side_send, side_recv, first_ready, shift_ready,
 ):
     segment = lax.axis_index("segment")
     tok = lax.axis_index("tok")
@@ -134,16 +126,37 @@
     def away(at, sign):
         return wrapped(x + sign * at[0], NX) * NY + wrapped(y + sign * at[1], NY)
 
-    for at in peers:
-        pl.semaphore_signal(barrier, inc=1, device_id=(segment, away(at, 1), half), device_id_type=MESH)
-
-    @pl.when(segment < last)
+    others = tok != 0
+
+    @pl.when(others)
+    def _():
+        for at in peers:
+            pl.semaphore_signal(barrier, inc=1, device_id=(segment, away(at, 1), half), device_id_type=MESH)
+
+    @pl.when(others & (segment < last))
     def _():
         pl.semaphore_signal(barrier, inc=1, device_id=(segment + 1, tok, half), device_id_type=MESH)
 
+    @pl.when((tok == 0) & (segment > 0))
+    def _():
+        pl.semaphore_signal(barrier, inc=1, device_id=(segment - 1, tok, half), device_id_type=MESH)
+
     @pl.when(half == 0)
     def _():
         pl.semaphore_signal(barrier, inc=1, device_id=(segment, tok, 1), device_id_type=MESH)
+
+    beside = jnp.where(others, (segment > 0).astype(jnp.int32), (segment < last).astype(jnp.int32))
+    entered = GROUP - 1 - others.astype(jnp.int32) + beside + half
+
+    @pl.when(tok == 0)
+    def _():
+        pl.semaphore_wait(barrier, entered)
+        for at in peers:
+            pl.semaphore_signal(first_ready, inc=1, device_id=(segment, away(at, 1), half), device_id_type=MESH)
+
+    @pl.when((tok == 0) & (segment < last))
+    def _():
+        pl.semaphore_signal(shift_ready, inc=1, device_id=(segment + 1, tok, half), device_id_type=MESH)
 
     for copy in loads[:3]:
         copy.wait()
@@ -168,18 +181,23 @@
         sent[2 * k] = jnp.where(low, top, pltpu.roll(bottom, WIDTH, 1)).astype(jnp.bfloat16)
         sent[2 * k + 1] = jnp.where(low, pltpu.roll(top, WIDTH, 1), bottom).astype(jnp.bfloat16)
 
-    pl.semaphore_wait(barrier, GROUP - 1 + (segment > 0).astype(jnp.int32) + half)
+    @pl.when(others)
+    def _():
+        pl.semaphore_wait(barrier, entered)
 
     def exchange(at, sign):
-        peer, i = away(at, sign), at[0] * NY + at[1]
+        peer = away(at, sign)
         return pltpu.make_async_remote_copy(
             src_ref=sent.at[peer if sign > 0 else tok], dst_ref=landed.at[tok if sign > 0 else peer],
-            send_sem=all_send.at[i], recv_sem=all_recv.at[i],
+            send_sem=all_send, recv_sem=all_recv,
             device_id=(segment, peer, half), device_id_type=MESH,
         )
 
     for at in peers:
-        exchange(at, 1).start()
+
+        @pl.when(away(at, 1) != 0)
+        def _():
+            exchange(at, 1).start()
 
     def previous(i, src, dst):
         return pltpu.make_async_remote_copy(
@@ -191,10 +209,17 @@
     loads[4].wait()
     weights = previous(1, router, next_router)
 
-    @pl.when(segment > 0)
+    @pl.when(others & (segment > 0))
     def _():
         whole.start()
         weights.start()
+
+    def late_shift():
+        @pl.when((tok == 0) & (segment > 0))
+        def _():
+            pl.semaphore_wait(shift_ready, 1)
+            whole.start()
+            weights.start()
 
     loads[3].wait()
     total = jnp.zeros((128, 128), jnp.float32)
@@ -232,8 +257,20 @@
         def _():
             scores.start()
 
-    for at in peers:
-        exchange(at, -1).wait_recv()
+    @pl.when(others)
+    def _():
+        pl.semaphore_wait(first_ready, 1)
+        pltpu.make_async_remote_copy(
+            src_ref=sent.at[0], dst_ref=landed.at[tok], send_sem=all_send, recv_sem=all_recv,
+            device_id=(segment, 0, half), device_id_type=MESH,
+        ).start()
+
+    every = pltpu.make_async_remote_copy(
+        src_ref=sent.at[pl.ds(0, GROUP - 1)], dst_ref=landed.at[pl.ds(0, GROUP - 1)],
+        send_sem=all_send, recv_sem=all_recv,
+        device_id=(segment, away((0, 1), 1), half), device_id_type=MESH,
+    )
+    every.wait_recv()
 
     got = landed[...].astype(jnp.float32)
     k24 = lax.broadcasted_iota(jnp.int32, (GROUP, HALF, 128), 1).astype(jnp.float32)
@@ -260,33 +297,33 @@
     steps, head, index, _ = ring_plan()
 
     def block(key, held):
-        c, stage, e, s, d = key
-        n = {("A", 1): NX, ("A", 2): NY, ("B", 1): NY, ("B", 2): NX}[(c, stage)]
-        back = s * (d - 1 + (1 if held else 0))
-        along = (x if n == NX else y) - back
+        c, u, stage, e, s, d = key
+        on_x = (c == "A") == (stage == 1)
+        along = (x if on_x else y) - s * (d if held else PARENT[c, stage][d])
         if stage == 1:
-            sx, sy = (along, y) if n == NX else (x, along)
-        elif c == "A":
-            sx, sy = x - e, along
+            sx, sy = (along, y) if on_x else (x, along)
         else:
-            sx, sy = along, y - e
+            sx, sy = (along, y - e) if on_x else (x - e, along)
         source = wrapped(sx, NX) * NY + wrapped(sy, NY)
         start, size = (0, ROWS_A) if c == "A" else (ROWS_A, WIDTH - ROWS_A)
         at = pl.ds(pl.multiple_of(source * WIDTH + start, 8), size)
-        if d < n // 2:
-            return rows.at[at]
-        return rows.at[at, pl.ds(0 if s == 1 else ACTIVE // 2, ACTIVE // 2)]
+        lanes = ACTIVE // SPLIT[c]
+        first = lanes * u
+        if d == (NX if on_x else NY) // 2:
+            lanes //= 2
+            first += 0 if s == 1 else lanes
+        return rows.at[at, pl.ds(first, lanes)]
 
     def ring(key, held):
-        c, stage, e, s, d = key
-        on_x = (c == "A") == (stage == 1)
-        if on_x:
-            to = wrapped(x + s, NX) * NY + y
+        c, u, stage, e, s, d = key
+        step = s * (d - PARENT[c, stage][d])
+        if (c == "A") == (stage == 1):
+            to = wrapped(x + step, NX) * NY + y
         else:
-            to = x * NY + wrapped(y + s, NY)
+            to = x * NY + wrapped(y + step, NY)
         ref = block(key, held)
         return pltpu.make_async_remote_copy(
-            src_ref=ref, dst_ref=ref, send_sem=ring_send.at[index[key]], recv_sem=ring_recv.at[index[key]],
+            src_ref=ref, dst_ref=ref, send_sem=ring_send, recv_sem=ring_recv.at[index[key]],
             device_id=(segment, to, half), device_id_type=MESH,
         )
 
@@ -307,6 +344,8 @@
             received_ref[...] = jnp.zeros_like(received_ref)
 
     for i, (what, key) in enumerate(steps):
+        if i == 12:
+            late_shift()
         if i == head // 4:
             answer()
         if i == head // 2:
@@ -325,11 +364,12 @@
         scores.wait_send()
 
     swap.wait_send()
-    for at in peers:
-        exchange(at, 1).wait_send()
-    for what, key in steps:
-        if what == "send":
-            ring(key, False).wait_send()
+    every.wait_send()
+    gone = rows.at[pl.ds(0, (GROUP - 1) * WIDTH)]
+    pltpu.make_async_remote_copy(
+        src_ref=gone, dst_ref=gone, send_sem=ring_send, recv_sem=ring_recv.at[0],
+        device_id=(segment, away((0, 1), 1), half), device_id_type=MESH,
+    ).wait_send()
 
 
 def finish(received_ref, rows, act, received_hbm, grad_hbm, grad, sems):
@@ -378,12 +418,14 @@
             pltpu.VMEM((8, 128), f32),
             pltpu.VMEM((1, 2048), f32),
             pltpu.SemaphoreType.DMA((5,)),
-            pltpu.SemaphoreType.DMA((GROUP,)),
-            pltpu.SemaphoreType.DMA((GROUP,)),
-            pltpu.SemaphoreType.DMA((messages,)),
+            pltpu.SemaphoreType.DMA,
+            pltpu.SemaphoreType.DMA,
+            pltpu.SemaphoreType.DMA,
             pltpu.SemaphoreType.DMA((messages,)),
             pltpu.SemaphoreType.DMA((4,)),
             pltpu.SemaphoreType.DMA((4,)),
+            pltpu.SemaphoreType.REGULAR,
+            pltpu.SemaphoreType.REGULAR,
         ],
         compiler_params=pltpu.CompilerParams(collective_id=0, has_side_effects=True, vmem_limit_bytes=48 << 20),
         cost_estimate=pl.CostEstimate(flops=20_000_000_000, bytes_accessed=2 << 20, transcendentals=0),

time: 49.5 us -> 45.8 us (0.925)
  the two profiles are of different devices: /device:TPU:8 before, /device:TPU:2 now
where the time goes in v3:
time: 45.8 us; the launch traced here: 45.6 us
  Pallas kernels  45 us (98%)
  between operations  0.66 us (1%)
    pallas_call x1, Pallas kernels, per_device(): pl.pallas_call(kernel, out_shape=(jax.ShapeDtypeStruct((128, 2048), bf16)...  42.9 us
    pallas_call x1, Pallas kernels, per_device(): pl.pallas_call(finish, out_shape=(jax.ShapeDtypeStruct((128, 2048), bf16)...  2.04 us

profile of v3, /device:TPU:2, one launch (start us, length us, event | category | flops | bytes accessed | tf_op | source)
XLA Modules:
  0.0 45.6 jit_solution(9657072255601093753)
XLA Ops:
  0.6 0.0 copy-start
  0.6 42.9 %shard_map.77 = (bf16[128,2048]{1,0:T(8,128)(2,1)S(1)}, bf16[2048,512]{1,0:T(8,128)(2,1)S(1)}) custom-call(bf16[128,2048]{1,0:T(8,128)(2,1)} %bitcast.10, bf16[128,2048]{1,0:T(8,128)(2,1)} %bitcast.11, f32[1,128]{1,0:T(1,128)} %logit_hbm.1, s32[1,128]{1,0:T(1,128)} %keep_hbm.1, f32[1,2048]{1,0:T(1,128)} %router_hbm.1), custom_call_target="tpu_custom_call" | custom-call | flops 20000000000 | bytes 2097152 | tf_op jit(solution)/shard_map/pallas_call | solution.py:401
  43.6 0.0 copy-done
  43.6 2.0 %shard_map.78 = (bf16[128,2048]{1,0:T(8,128)(2,1)}, bf16[448,2048]{1,0:T(8,128)(2,1)}) custom-call(bf16[128,2048]{1,0:T(8,128)(2,1)S(1)} %get-tuple-element.6.received_ref, bf16[2048,512]{1,0:T(8,128)(2,1)S(1)} %get-tuple-element.7.rows, bf16[448,512]{1,0:T(8,128)(2,1)S(1)} %bitcast.9), custom_call_target="tpu_custom_call" | custom-call | flops 1000000000 | bytes 5242880 | tf_op jit(solution)/shard_map/pallas_call | solution.py:433
Async XLA Ops:
  0.6 42.9 %copy-start = (bf16[1,512,448]{1,2,0:T(8,128)(2,1)S(1)}, bf16[1,512,448]{1,2,0:T(8,128)(2,1)}, u32[]{:S(2)}) copy-start(bf16[1,512,448]{1,2,0:T(8,128)(2,1)} %param.11) | copy-start | bytes 1376260

commit v4 on v3

--- a/solution.py
+++ b/solution.py
@@ -17,6 +17,7 @@
 ACTIVE = 512
 
 
+LATE = 3.0
 SPLIT = {"A": 2, "B": 2}
 PARENT = {
     ("A", 1): {1: 0, 2: 1},
@@ -28,7 +29,7 @@
 
 @functools.cache
 def ring_plan():
-    rate, latency, hop = 46.6e3, 2.6, 0.75
+    rate, latency, hop = 46.6e3, 3.7, 0.75
     size = {"A": ROWS_A * 1024 / SPLIT["A"], "B": (WIDTH - ROWS_A) * 1024 / SPLIT["B"]}
     messages, needs = {}, {}
     for c in "AB":
@@ -78,16 +79,21 @@
         arrived[key] = free[link(key)] + latency + hop * (hops - 1)
         order.append((start, key))
         pending.remove(key)
-    steps, done = [], set()
-    for start, key in sorted(order, key=lambda item: item[0]):
-        for k in needs[key]:
-            if k not in done:
-                done.add(k)
-                steps.append(("wait", k))
-        steps.append(("send", key))
-    head = len(steps)
-    steps += [("wait", k) for k in sorted((k for k in messages if k not in done), key=lambda k: arrived[k])]
-    return steps, head, {k: i for i, k in enumerate(sorted(messages))}, max(arrived.values())
+    items = []
+    for late in (False, True):
+        done = set()
+        for start, key in sorted(order, key=lambda item: item[0]):
+            fresh = tuple(k for k in needs[key] if k not in done)
+            done.update(fresh)
+            if needs[key]:
+                items.append((start + (LATE if late else 0.0), late, fresh, key))
+            elif not late:
+                items.append((start, None, (), key))
+    items.sort(key=lambda item: item[0])
+    passed = [k for k in sorted(messages) if k in done]
+    ends = [k for k in messages if k not in done]
+    index = {k: i for i, k in enumerate(passed)} | {k: len(passed) for k in ends}
+    return items, index, int(sum(messages[k][0] for k in ends)), max(arrived.values())
 
 
 def wrapped(value, n):
@@ -294,9 +300,9 @@
         tile += jnp.dot(flipped[WIDTH:], pick_bottom, preferred_element_type=jnp.float32)
         rows[pl.ds(own, WIDTH), 128 * t : 128 * (t + 1)] = tile.astype(jnp.bfloat16)
 
-    steps, head, index, _ = ring_plan()
-
-    def block(key, held):
+    items, index, end_bytes, _ = ring_plan()
+
+    def origin(key, held):
         c, u, stage, e, s, d = key
         on_x = (c == "A") == (stage == 1)
         along = (x if on_x else y) - s * (d if held else PARENT[c, stage][d])
@@ -304,7 +310,12 @@
             sx, sy = (along, y) if on_x else (x, along)
         else:
             sx, sy = (along, y - e) if on_x else (x - e, along)
-        source = wrapped(sx, NX) * NY + wrapped(sy, NY)
+        return wrapped(sx, NX) * NY + wrapped(sy, NY)
+
+    def block(key, held):
+        c, u, stage, e, s, d = key
+        on_x = (c == "A") == (stage == 1)
+        source = origin(key, held)
         start, size = (0, ROWS_A) if c == "A" else (ROWS_A, WIDTH - ROWS_A)
         at = pl.ds(pl.multiple_of(source * WIDTH + start, 8), size)
         lanes = ACTIVE // SPLIT[c]
@@ -343,19 +354,29 @@
         def _():
             received_ref[...] = jnp.zeros_like(received_ref)
 
-    for i, (what, key) in enumerate(steps):
-        if i == 12:
-            late_shift()
-        if i == head // 4:
-            answer()
-        if i == head // 2:
-            tell()
-        if i == head:
-            receive()
-        if what == "send":
+    extra = [(1.2, late_shift), (4.5, answer), (8.0, tell)]
+    for when, late, waits, key in items:
+        while extra and extra[0][0] <= when:
+            extra.pop(0)[1]()
+        if late is None:
             ring(key, False).start()
-        else:
-            ring(key, True).wait_recv()
+            continue
+        source = origin(key, False)
+
+        @pl.when(source == 0 if late else source != 0)
+        def _():
+            for k in waits:
+                ring(k, True).wait_recv()
+            ring(key, False).start()
+
+    for _, act_now in extra:
+        act_now()
+    receive()
+    came = rows.at[pl.ds(0, end_bytes // (2 * ACTIVE))]
+    pltpu.make_async_remote_copy(
+        src_ref=came, dst_ref=came, send_sem=ring_send, recv_sem=ring_recv.at[max(index.values())],
+        device_id=(segment, away((0, 1), 1), half), device_id_type=MESH,
+    ).wait_recv()
 
     @pl.when(segment > 0)
     def _():
@@ -392,7 +413,7 @@
 def per_device(out_cotangent, block_output, router_logits, keep_flags, router_weight, activated):
     anywhere = pl.BlockSpec(memory_space=pltpu.HBM)
     inside = pl.BlockSpec(memory_space=pltpu.VMEM)
-    messages = len(ring_plan()[2])
+    messages = 1 + max(ring_plan()[1].values())
     bf16, f32 = jnp.bfloat16, jnp.float32
     far = [
         pltpu.with_memory_space_constraint(a, pltpu.HBM)

time: 45.8 us -> 43.3 us (0.945)
  Pallas kernels: 45 us -> 42.5 us
    pallas_call x1, Pallas kernels: 42.9 us -> 40.5 us  [per_device(): pl.pallas_call(kernel, out_shape=(jax.ShapeDtypeStruct((128, 2048), bf16)...]
where the time goes in v4:
time: 43.3 us; the launch traced here: 43.2 us
  Pallas kernels  42.5 us (98%)
  between operations  0.66 us (2%)
    pallas_call x1, Pallas kernels, per_device(): pl.pallas_call(kernel, out_shape=(jax.ShapeDtypeStruct((128, 2048), bf16)...  40.5 us
    pallas_call x1, Pallas kernels, per_device(): pl.pallas_call(finish, out_shape=(jax.ShapeDtypeStruct((128, 2048), bf16)...  2.04 us

profile of v4, /device:TPU:2, one launch (start us, length us, event | category | flops | bytes accessed | tf_op | source)
XLA Modules:
  0.0 43.2 jit_solution(1758436372390383949)
XLA Ops:
  0.6 0.0 copy-start
  0.6 40.5 %shard_map.77 = (bf16[128,2048]{1,0:T(8,128)(2,1)S(1)}, bf16[2048,512]{1,0:T(8,128)(2,1)S(1)}) custom-call(bf16[128,2048]{1,0:T(8,128)(2,1)} %bitcast.10, bf16[128,2048]{1,0:T(8,128)(2,1)} %bitcast.11, f32[1,128]{1,0:T(1,128)} %logit_hbm.1, s32[1,128]{1,0:T(1,128)} %keep_hbm.1, f32[1,2048]{1,0:T(1,128)} %router_hbm.1), custom_call_target="tpu_custom_call" | custom-call | flops 20000000000 | bytes 2097152 | tf_op jit(solution)/shard_map/pallas_call | solution.py:422
  41.1 0.0 copy-done
  41.1 2.0 %shard_map.78 = (bf16[128,2048]{1,0:T(8,128)(2,1)}, bf16[448,2048]{1,0:T(8,128)(2,1)}) custom-call(bf16[128,2048]{1,0:T(8,128)(2,1)S(1)} %get-tuple-element.6.received_ref, bf16[2048,512]{1,0:T(8,128)(2,1)S(1)} %get-tuple-element.7.rows, bf16[448,512]{1,0:T(8,128)(2,1)S(1)} %bitcast.9), custom_call_target="tpu_custom_call" | custom-call | flops 1000000000 | bytes 5242880 | tf_op jit(solution)/shard_map/pallas_call | solution.py:454
Async XLA Ops:
  0.6 40.5 %copy-start = (bf16[1,512,448]{1,2,0:T(8,128)(2,1)S(1)}, bf16[1,512,448]{1,2,0:T(8,128)(2,1)}, u32[]{:S(2)}) copy-start(bf16[1,512,448]{1,2,0:T(8,128)(2,1)} %param.11) | copy-start | bytes 1376260

commit v5 on v4

--- a/solution.py
+++ b/solution.py
@@ -35,6 +35,7 @@
     for c in "AB":
         n, m = (NX, NY) if c == "A" else (NY, NX)
         for u in range(SPLIT[c]):
+            side = 1 - 2 * (u % 2)
             for stage, ring, offsets in ((1, n, (0,)), (2, m, range(n))):
                 for e in offsets:
                     if stage == 1 or e == 0:
@@ -44,11 +45,11 @@
                     elif e > n // 2:
                         base = [(c, u, 1, 0, -1, n - e)]
                     else:
-                        base = [(c, u, 1, 0, 1, e), (c, u, 1, 0, -1, e)]
+                        base = [(c, u, 1, 0, side, e)]
                     for s in (1, -1):
-                        for d in range(1, ring // 2 + 1):
+                        for d in range(1, ring // 2 + (1 if s == side else 0)):
                             key, parent = (c, u, stage, e, s, d), PARENT[c, stage][d]
-                            messages[key] = (size[c] * (0.5 if d == ring // 2 else 1.0), d - parent)
+                            messages[key] = (size[c], d - parent)
                             needs[key] = [(c, u, stage, e, s, parent)] if parent else base
     after = {key: [] for key in messages}
     for key in messages:
@@ -314,16 +315,11 @@
 
     def block(key, held):
         c, u, stage, e, s, d = key
-        on_x = (c == "A") == (stage == 1)
         source = origin(key, held)
         start, size = (0, ROWS_A) if c == "A" else (ROWS_A, WIDTH - ROWS_A)
         at = pl.ds(pl.multiple_of(source * WIDTH + start, 8), size)
         lanes = ACTIVE // SPLIT[c]
-        first = lanes * u
-        if d == (NX if on_x else NY) // 2:
-            lanes //= 2
-            first += 0 if s == 1 else lanes
-        return rows.at[at, pl.ds(first, lanes)]
+        return rows.at[at, pl.ds(lanes * u, lanes)]
 
     def ring(key, held):
         c, u, stage, e, s, d = key

time: 43.3 us -> 42.7 us (0.986)
  the two profiles are of different devices: /device:TPU:2 before, /device:TPU:8 now
where the time goes in v5:
time: 42.7 us; the launch traced here: 42.5 us
  Pallas kernels  41.9 us (98%)
  between operations  0.66 us (2%)
    pallas_call x1, Pallas kernels, per_device(): pl.pallas_call(kernel, out_shape=(jax.ShapeDtypeStruct((128, 2048), bf16)...  39.8 us
    pallas_call x1, Pallas kernels, per_device(): pl.pallas_call(finish, out_shape=(jax.ShapeDtypeStruct((128, 2048), bf16)...  2.04 us

profile of v5, /device:TPU:8, one launch (start us, length us, event | category | flops | bytes accessed | tf_op | source)
XLA Modules:
  0.0 42.5 jit_solution(11262011495971995446)
XLA Ops:
  0.6 0.0 copy-start
  0.6 39.8 %shard_map.77 = (bf16[128,2048]{1,0:T(8,128)(2,1)S(1)}, bf16[2048,512]{1,0:T(8,128)(2,1)S(1)}) custom-call(bf16[128,2048]{1,0:T(8,128)(2,1)} %bitcast.10, bf16[128,2048]{1,0:T(8,128)(2,1)} %bitcast.11, f32[1,128]{1,0:T(1,128)} %logit_hbm.1, s32[1,128]{1,0:T(1,128)} %keep_hbm.1, f32[1,2048]{1,0:T(1,128)} %router_hbm.1), custom_call_target="tpu_custom_call" | custom-call | flops 20000000000 | bytes 2097152 | tf_op jit(solution)/shard_map/pallas_call | solution.py:418
  40.5 0.0 copy-done
  40.5 2.0 %shard_map.78 = (bf16[128,2048]{1,0:T(8,128)(2,1)}, bf16[448,2048]{1,0:T(8,128)(2,1)}) custom-call(bf16[128,2048]{1,0:T(8,128)(2,1)S(1)} %get-tuple-element.6.received_ref, bf16[2048,512]{1,0:T(8,128)(2,1)S(1)} %get-tuple-element.7.rows, bf16[448,512]{1,0:T(8,128)(2,1)S(1)} %bitcast.9), custom_call_target="tpu_custom_call" | custom-call | flops 1000000000 | bytes 5242880 | tf_op jit(solution)/shard_map/pallas_call | solution.py:450
Async XLA Ops:
  0.6 39.9 %copy-start = (bf16[1,512,448]{1,2,0:T(8,128)(2,1)S(1)}, bf16[1,512,448]{1,2,0:T(8,128)(2,1)}, u32[]{:S(2)}) copy-start(bf16[1,512,448]{1,2,0:T(8,128)(2,1)} %param.11) | copy-start | bytes 1376260
